TPU v7x, 32 devices: a whole 2x2x4 slice. The times are simulated.
32 devices in a mesh: row: 8 (over z, x), col: 4 (over y, core).
Axes of the slice: x: 2, y: 2, z: 4, core: 2. Of those that a mesh axis runs over, the one named last changes fastest.
Arguments:
- visible_data: bfloat16 [512, 32768], P('col', 'row'), may hold values from 0 to 1
- hidden_uniform: float32 [512, 16384], P('row', 'col'), may hold values from 0.01 to 0.99
- visible_uniform: float32 [512, 32768], P('col', 'row'), may hold values from 0.01 to 0.99
- weights: bfloat16 [32768, 16384], P('row', 'col'), may hold values from -0.03125 to 0.03125
- visible_bias: float32 [32768], P('row'), may hold values from -4 to 4
- hidden_bias: float32 [16384], P('col'), may hold values from -4 to 4
Outputs:
- grad_weights: bfloat16 [32768, 16384], P('row', 'col')
- grad_visible: float32 [32768], P('row')
- grad_hidden: float32 [16384], P('col')
- hidden_sample: bfloat16 [512, 16384], P('row', 'col')
- reconstruction: bfloat16 [512, 32768], P('col', 'row')
All inputs are finite; a program needn't handle non-finite values.
Results may differ from a plain program's by a relative error of at most 0.0034.
Values may be sent and summed in bfloat16 or wider, within the bound.
A program may use at most 192 MiB of HBM per device.

v0:
```python
import jax
import jax.numpy as jnp
from jax import lax
from jax.sharding import PartitionSpec as P


def relaxed(field, uniform):
    return jax.nn.sigmoid(2.0 * (field + jnp.log(uniform) - jnp.log1p(-uniform)))


def scatter_sum(partial_value, axis):
    narrow = partial_value.astype(jnp.bfloat16)
    return lax.psum_scatter(narrow, axis, scatter_dimension=0, tiled=True).astype(jnp.float32)


def gather(value, axis):
    return lax.all_gather(value, axis, axis=0, tiled=True)


def on_device(visible_data, hidden_uniform, visible_uniform, weights, visible_bias, hidden_bias):
    batch_total = visible_data.shape[0] * lax.axis_size("col")
    transposed = (((1,), (1,)), ((), ()))
    contract_batch = (((0,), (0,)), ((), ()))
    visible_full = gather(visible_data, "col")

    def hidden_field(source):
        partial_value = jnp.dot(source, weights, preferred_element_type=jnp.float32)
        return scatter_sum(partial_value, "row") + hidden_bias

    field_pos = hidden_field(visible_full)
    probs_pos = jax.nn.sigmoid(field_pos).astype(jnp.bfloat16)
    sample_own = relaxed(field_pos, hidden_uniform).astype(jnp.bfloat16)
    sample_full = gather(sample_own, "row")
    visible_partial = lax.dot_general(
        sample_full, weights, transposed, preferred_element_type=jnp.float32
    )
    field_neg = scatter_sum(visible_partial, "col") + visible_bias
    recon_own = relaxed(field_neg, visible_uniform).astype(jnp.bfloat16)
    recon_full = gather(recon_own, "col")
    probs_full = gather(probs_pos, "row")
    probs_back = jax.nn.sigmoid(hidden_field(recon_full)).astype(jnp.bfloat16)
    negative_full = gather(probs_back, "row")
    left_side = jnp.concatenate([visible_full, recon_full], axis=0)
    right_side = jnp.concatenate([probs_full, -negative_full], axis=0)
    difference = lax.dot_general(
        left_side, right_side, contract_batch, preferred_element_type=jnp.float32
    )
    grad_weights = (difference / batch_total).astype(jnp.bfloat16)
    grad_visible = jnp.mean(
        visible_full.astype(jnp.float32) - recon_full.astype(jnp.float32), axis=0
    )
    grad_hidden = jnp.mean(
        probs_full.astype(jnp.float32) - negative_full.astype(jnp.float32), axis=0
    )
    return (grad_weights, grad_visible, grad_hidden, sample_own, recon_own)


def solution(mesh):
    placed = (
        P("col", "row"),
        P("row", "col"),
        P("col", "row"),
        P("row", "col"),
        P("row"),
        P("col"),
    )
    return jax.shard_map(
        on_device,
        mesh=mesh,
        in_specs=placed,
        out_specs=(P("row", "col"), P("row"), P("col"), P("row", "col"), P("col", "row")),
        check_vma=False,
    )
```

profile of v0, /device:TPU:0, one launch (start us, length us, event | category | flops | bytes accessed | tf_op | source)
XLA Modules:
  0.0 658.9 jit_solution(7479944351545597440)
XLA Ops:
  7.2 0.0 all-gather.6.cloned.1.call-start
  7.2 0.7 all-gather.6.cloned.1.call-update
  7.9 0.0 reduce-scatter.4.cloned.1.call-start
  7.9 38.8 %all-gather.6.cloned.1.call-done = bf16[512,4096]{1,0:T(8,128)(2,1)} async-done(((bf16[128,4096]{1,0:T(8,128)(2,1)}), bf16[512,4096]{1,0:T(8,128)(2,1)}) %all-gather.6.cloned.1.call-update) | async-done | bytes 4194320 | tf_op jit(solution)/shard_map/all_gather | solution.py:17
  46.8 23.6 %convolution_convert_fusion.2 = bf16[512,4096]{1,0:T(8,128)(2,1)} fusion(bf16[512,4096]{1,0:T(8,128)(2,1)} %all-gather.6.cloned.1.call-done, bf16[4096,4096]{1,0:T(8,128)(2,1)} %param.9), kind=kOutput, calls=%fused_computation.11 | convolution fusion | flops 17181966336 | bytes 41943040 | tf_op jit(solution)/shard_map/dot_general | solution.py:27
  70.3 0.0 reduce-scatter.4.cloned.1.call-update
  70.3 0.0 all-gather.8.cloned.1.call-start
  70.4 88.4 %reduce-scatter.4.cloned.1.call-done = bf16[64,4096]{1,0:T(8,128)(2,1)} async-done(((bf16[512,4096]{1,0:T(8,128)(2,1)}), bf16[64,4096]{1,0:T(8,128)(2,1)}) %reduce-scatter.4.cloned.1.call-update) | async-done | bytes 524304 | tf_op jit(solution)/shard_map/reduce_scatter | solution.py:13
  158.8 2.9 divide_convert_fusion.2
  161.7 0.0 all-gather.8.cloned.1.call-update
  161.7 0.0 reduce-scatter.6.cloned.1.call-start
  161.8 72.5 %all-gather.8.cloned.1.call-done = bf16[512,4096]{1,0:T(8,128)(2,1)} async-done(((bf16[64,4096]{1,0:T(8,128)(2,1)}), bf16[512,4096]{1,0:T(8,128)(2,1)}) %all-gather.8.cloned.1.call-update) | async-done | bytes 4194320 | tf_op jit(solution)/shard_map/all_gather | solution.py:17
  234.3 23.7 %convolution_convert_fusion.1 = bf16[512,4096]{1,0:T(8,128)(2,1)} fusion(bf16[512,4096]{1,0:T(8,128)(2,1)} %all-gather.8.cloned.1.call-done, bf16[4096,4096]{1,0:T(8,128)(2,1)} %param.9), kind=kOutput, calls=%fused_computation.10 | convolution fusion | flops 17181966336 | bytes 41943040 | tf_op jit(solution)/shard_map/dot_general | solution.py:34
  258.0 0.0 all-gather.10.cloned.1.call-start
  258.0 43.2 %reduce-scatter.6.cloned.1.call-done = bf16[128,4096]{1,0:T(8,128)(2,1)} async-done(((bf16[512,4096]{1,0:T(8,128)(2,1)}), bf16[128,4096]{1,0:T(8,128)(2,1)}) %reduce-scatter.6.cloned.1.call-update) | async-done | bytes 1048592 | tf_op jit(solution)/shard_map/reduce_scatter | solution.py:13
  301.3 3.7 divide_convert_fusion
  305.0 0.2 reduce-scatter.8.cloned.1.call-start
  305.2 34.4 %all-gather.10.cloned.1.call-done = bf16[512,4096]{1,0:T(8,128)(2,1)} async-done(((bf16[128,4096]{1,0:T(8,128)(2,1)}), bf16[512,4096]{1,0:T(8,128)(2,1)}) %all-gather.10.cloned.1.call-update) | async-done | bytes 4194320 | tf_op jit(solution)/shard_map/all_gather | solution.py:17
  339.6 23.6 %convolution_convert_fusion = bf16[512,4096]{1,0:T(8,128)(2,1)} fusion(bf16[512,4096]{1,0:T(8,128)(2,1)} %all-gather.10.cloned.1.call-done, bf16[4096,4096]{1,0:T(8,128)(2,1)} %param.9), kind=kOutput, calls=%fused_computation.9 | convolution fusion | flops 17181966336 | bytes 41943040 | tf_op jit(solution)/shard_map/dot_general | solution.py:27
  363.2 0.0 all-gather.12.cloned.1.call-start
  363.2 0.7 all-gather.12.cloned.1.call-update
  363.9 0.0 all-gather.14.cloned.1.call-start
  364.0 87.7 %reduce-scatter.8.cloned.1.call-done = bf16[64,4096]{1,0:T(8,128)(2,1)} async-done(((bf16[512,4096]{1,0:T(8,128)(2,1)}), bf16[64,4096]{1,0:T(8,128)(2,1)}) %reduce-scatter.8.cloned.1.call-update) | async-done | bytes 524304 | tf_op jit(solution)/shard_map/reduce_scatter | solution.py:13
  451.6 2.1 divide_convert_fusion.1
  453.7 4.9 subtract_reduce_fusion.1
  458.7 0.6 broadcast_multiply_fusion.1
  459.3 66.9 %all-gather.12.cloned.1.call-done = bf16[512,4096]{1,0:T(8,128)(2,1)} async-done(((bf16[64,4096]{1,0:T(8,128)(2,1)}), bf16[512,4096]{1,0:T(8,128)(2,1)}) %all-gather.12.cloned.1.call-update) | async-done | bytes 4194320 | tf_op jit(solution)/shard_map/all_gather | solution.py:17
  526.2 74.1 %all-gather.14.cloned.1.call-done = bf16[512,4096]{1,0:T(8,128)(2,1)} async-done(((bf16[64,4096]{1,0:T(8,128)(2,1)}), bf16[512,4096]{1,0:T(8,128)(2,1)}) %all-gather.14.cloned.1.call-update) | async-done | bytes 4194320 | tf_op jit(solution)/shard_map/all_gather | solution.py:17
  600.2 5.1 subtract_reduce_fusion
  605.3 0.6 broadcast_multiply_fusion
  605.9 2.8 neg.27
  608.7 43.4 %multiply_convert_fusion = bf16[4096,4096]{1,0:T(8,128)(2,1)} fusion(bf16[512,4096]{1,0:T(8,128)(2,1)} %all-gather.10.cloned.1.call-done, bf16[512,4096]{1,0:T(8,128)(2,1)} %all-gather.6.cloned.1.call-done, bf16[512,4096]{1,0:T(8,128)(2,1)} %neg.27, bf16[512,4096]{1,0:T(8,128)(2,1)} %all-gather.12.cloned.1.call-done), kind=kOutput, calls=%fused_computation | convolution fusion | flops 34426847232 | bytes 50331648 | tf_op jit(solution)/shard_map/dot_general | solution.py:45
  (14 shorter events, 0.1 us)
Async XLA Ops:
  7.2 39.6 %all-gather.6.cloned.1.call-start = ((), (), s32[]{:S(2)}) async-start(), calls=%async_computation.3 | async-start | bytes 5242880 | tf_op jit(solution)/shard_map/all_gather | solution.py:17
  7.9 150.9 %reduce-scatter.4.cloned.1.call-start = ((), (), s32[]{:S(2)}) async-start(), calls=%async_computation.4 | async-start | bytes 4718592 | tf_op jit(solution)/shard_map/reduce_scatter | solution.py:13
  70.3 88.5 %copy-start.2 = (f32[64,4096]{1,0:T(8,128)S(1)}, f32[64,4096]{1,0:T(8,128)}, u32[]{:S(2)}) copy-start(f32[64,4096]{1,0:T(8,128)} %param.7) | copy-start | bytes 3145732
  70.3 88.5 %copy-start.3 = (f32[4096]{0:T(1024)S(1)}, f32[4096]{0:T(1024)}, u32[]{:S(2)}) copy-start(f32[4096]{0:T(1024)} %param.11) | copy-start | bytes 49156
  70.3 163.9 %all-gather.8.cloned.1.call-start = ((), (), s32[]{:S(2)}) async-start(), calls=%async_computation.5 | async-start | bytes 4718592 | tf_op jit(solution)/shard_map/all_gather | solution.py:17
  161.7 139.5 %reduce-scatter.6.cloned.1.call-start = ((), (), s32[]{:S(2)}) async-start(), calls=%async_computation.6 | async-start | bytes 5242880 | tf_op jit(solution)/shard_map/reduce_scatter | solution.py:13
  258.0 43.3 %copy-start.1 = (f32[128,4096]{1,0:T(8,128)S(1)}, f32[128,4096]{1,0:T(8,128)}, u32[]{:S(2)}) copy-start(f32[128,4096]{1,0:T(8,128)} %param.8) | copy-start | bytes 6291460
  258.0 43.3 %copy-start.4 = (f32[4096]{0:T(1024)S(1)}, f32[4096]{0:T(1024)}, u32[]{:S(2)}) copy-start(f32[4096]{0:T(1024)} %param.10) | copy-start | bytes 49156
  258.0 81.6 %all-gather.10.cloned.1.call-start = ((), (), s32[]{:S(2)}) async-start(), calls=%async_computation.7 | async-start | bytes 5242880 | tf_op jit(solution)/shard_map/all_gather | solution.py:17
  305.0 146.7 %reduce-scatter.8.cloned.1.call-start = ((), (), s32[]{:S(2)}) async-start(), calls=%async_computation.9 | async-start | bytes 4718592 | tf_op jit(solution)/shard_map/reduce_scatter | solution.py:13
  363.2 163.0 %all-gather.12.cloned.1.call-start = ((), (), s32[]{:S(2)}) async-start(), calls=%async_computation.8 | async-start | bytes 4718592 | tf_op jit(solution)/shard_map/all_gather | solution.py:17
  363.9 236.3 %all-gather.14.cloned.1.call-start = ((), (), s32[]{:S(2)}) async-start(), calls=%async_computation.10 | async-start | bytes 4718592 | tf_op jit(solution)/shard_map/all_gather | solution.py:17
  600.2 5.7 copy-start
Sparse Core Ops, SparseCore 0:
  9.5 37.1 all-gather.5
  70.5 88.2 reduce-scatter.3
  161.8 72.3 all-gather.7
  258.1 43.1 reduce-scatter.5
  305.1 34.4 all-gather.9
  363.3 88.2 reduce-scatter.7
  453.7 72.3 all-gather.11
  528.9 71.3 all-gather.13
where the time goes:
time: 659 us
  waiting for transfers between devices  507 us (77%)
  matrix products  114 us (17%)
  other arithmetic  22.6 us (3%)
  between operations  14.2 us (2%)
    all_gather x5, waiting for transfers between devices, gather(): return lax.all_gather(value, axis, axis=0, tiled=True)  287 us
    reduce_scatter x3, waiting for transfers between devices, scatter_sum(): lax.psum_scatter(narrow, axis, scatter_dimension=0, tiled=True)  219 us
    dot_general x2, matrix products, hidden_field(): partial_value = jnp.dot(source, weights, preferred_element_type=jnp.float32)  47.1 us
    dot_general x1, matrix products, on_device(): lax.dot_general(left_side, right_side, contract_batch, preferred_element_...  43.4 us
    dot_general x1, matrix products, on_device(): lax.dot_general(sample_full, weights, transposed, preferred_element_type=...  23.7 us
  transfers between devices with their start and end apart: 8, of which 8 were waited for; matrix products, arithmetic and copies ran while one was open for 1% of the time, Pallas kernels for 0%

commit v1 on v0

v1 whole, which is shorter than its diff:
```python
import functools

import jax
import jax.numpy as jnp
from jax import lax
from jax.experimental import pallas as pl
from jax.experimental.pallas import tpu as pltpu
from jax.sharding import PartitionSpec as P

MESH = pl.DeviceIdType.MESH
BF16 = jnp.bfloat16
F32 = jnp.float32
ANY = pl.BlockSpec(memory_space=pl.ANY)
VM = pl.BlockSpec(memory_space=pltpu.VMEM)
LIMIT = 64_000_000


def sigmoid(t):
    return 1.0 / (1.0 + jnp.exp(-t))


def relaxed(field, uniform):
    return sigmoid(2.0 * (field + jnp.log(uniform) - jnp.log(1.0 - uniform)))


def col_tile(size, want):
    return min(size, want)


class Ring:
    def __init__(self, n):
        self.n = n
        me = lax.axis_index("row")
        self.me = me
        self.col = lax.axis_index("col")
        half, odd = me // 2, me % 2
        self.pos = half + odd * (n - 1 - 2 * half)
        self.right = self.index(self.pos + 1)
        self.left = self.index(self.pos + n - 1)

    def index(self, p):
        p = lax.rem(p, self.n)
        far = p // (self.n // 2)
        return (1 - far) * (2 * p) + far * (2 * (self.n - 1 - p) + 1)

    def peer(self, d):
        return (self.right if d == 0 else self.left, self.col)

    def rs_chunk(self, d, step):
        if d == 0:
            return self.index(self.pos + 2 * self.n - 1 - step)
        return self.index(self.pos + 1 + step)

    def ag_chunk(self, d, step):
        if d == 0:
            return self.index(self.pos + self.n - step)
        return self.index(self.pos + step)


class Group:
    def __init__(self, m):
        self.m = m
        self.chips = m // 2
        self.me = lax.axis_index("col")
        self.row = lax.axis_index("row")
        self.chip, self.core = self.me // 2, self.me % 2
        self.partner = (self.row, 2 * self.chip + 1 - self.core)

    def chip_at(self, offset):
        return lax.rem(self.chip + offset, self.chips)

    def peer(self, offset):
        return (self.row, 2 * self.chip_at(offset) + self.core)


def barrier(devices):
    sem = pltpu.get_barrier_semaphore()
    for device in devices:
        pl.semaphore_signal(sem, inc=1, device_id=device, device_id_type=MESH)
    pl.semaphore_wait(sem, len(devices))


def remote(src, dst, send, recv, device):
    return pltpu.make_async_remote_copy(
        src_ref=src, dst_ref=dst, send_sem=send, recv_sem=recv, device_id=device, device_id_type=MESH
    )


def cols(start, width):
    return pl.ds(pl.multiple_of(start, 128), width)


def ring_field(ring, x2d, w_hbm, wbuf, wsem, part, recv, gath, rs_sem, ag_sem, ssem, finish, consume):
    n = ring.n
    h = part.shape[2]
    nt = wbuf.shape[2]
    tiles = h // nt
    w = nt // 2
    last = 2 * n - 2

    def load(t):
        return pltpu.make_async_copy(
            w_hbm.at[:, cols(t * nt, nt)], wbuf.at[lax.rem(t, 2)], wsem.at[lax.rem(t, 2)]
        )

    def rs(t, d, step):
        area = cols(t * nt + d * w, w)
        return remote(
            part.at[ring.rs_chunk(d, step), :, area],
            recv.at[step, :, area],
            ssem.at[t, d],
            rs_sem.at[t, d, step],
            ring.peer(d),
        )

    def ag(t, d, step):
        area = cols(t * nt + d * w, w)
        chunk = ring.ag_chunk(d, step)
        return remote(
            gath.at[chunk, :, area], gath.at[chunk, :, area], ssem.at[t, d], ag_sem.at[t, d, step], ring.peer(d)
        )

    def slot(k, carry):
        @pl.when(k < tiles)
        def _():
            load(k).wait()

            @pl.when(k + 1 < tiles)
            def _():
                load(k + 1).start()

            sub = min(nt, 256)

            def piece(i, c):
                value = jnp.dot(
                    x2d(), wbuf[lax.rem(k, 2), :, cols(i * sub, sub)], preferred_element_type=F32
                )
                part[:, :, cols(k * nt + i * sub, sub)] = value.astype(BF16).reshape(n, part.shape[1], sub)
                return c

            lax.fori_loop(0, nt // sub, piece, 0)
            for d in range(2):
                rs(k, d, 0).start()

        def tile(t, c):
            j = k - t

            @pl.when((j >= 1) & (j <= n - 2))
            def _():
                for d in range(2):
                    area = cols(t * nt + d * w, w)
                    rs(t, d, j - 1).wait()
                    q = ring.rs_chunk(d, j)
                    total = part[q, :, area].astype(F32) + recv[j - 1, :, area].astype(F32)
                    part[q, :, area] = total.astype(BF16)
                    rs(t, d, j).start()

            @pl.when(j == n - 1)
            def _():
                for d in range(2):
                    area = cols(t * nt + d * w, w)
                    rs(t, d, n - 2).wait()
                    total = part[ring.me, :, area].astype(F32) + recv[n - 2, :, area].astype(F32)
                    gath[ring.me, :, area] = finish(area, total)
                    ag(t, d, 0).start()

            @pl.when((j >= n) & (j <= 2 * n - 3))
            def _():
                for d in range(2):
                    ag(t, d, j - n).wait()
                    ag(t, d, j - n + 1).start()

            @pl.when(j == last)
            def _():
                for d in range(2):
                    ag(t, d, n - 2).wait()

            return c

        lax.fori_loop(jnp.maximum(k - last, 0), jnp.minimum(k + 1, tiles), tile, 0)
        if consume is not None:

            @pl.when(k == last - 1)
            def _():
                load(0).start()

            @pl.when(k >= last)
            def _():
                t = k - last
                load(t).wait()

                @pl.when(t + 1 < tiles)
                def _():
                    load(t + 1).start()

                consume(t)

        return carry

    lax.fori_loop(0, tiles + last, slot, 0)


def positive_kernel(
    n, m, vis, w_hbm, uni, bias, sample_out, probs_out, part2_out, vis_out,
    x, wbuf, part, recv, gath, acc, narrow, wsem, rs_sem, ag_sem, ssem, own_sem, gs, gr, fs, fr, out_sem,
):
    ring, group = Ring(n), Group(m)
    rows_c = x.shape[1]
    batch = m * rows_c
    v = x.shape[2]
    nt = wbuf.shape[2]
    pltpu.make_async_copy(w_hbm.at[:, cols(0, nt)], wbuf.at[0], wsem.at[0]).start()
    own = pltpu.make_async_copy(vis, x.at[group.me], own_sem)
    own.start()
    offsets = range(1, group.chips)
    barrier([ring.peer(0), ring.peer(1), group.partner] + [group.peer(o) for o in offsets])
    own.wait()
    sends = [
        remote(x.at[group.me], x.at[group.me], gs.at[o - 1], gr.at[o - 1], group.peer(o)) for o in offsets
    ]
    for copy in sends:
        copy.start()
    mine = remote(x.at[group.me], x.at[group.me], fs.at[0], fr.at[0], group.partner)
    mine.start()
    forwards = []
    for o in offsets:
        sends[o - 1].wait()
        block = 2 * group.chip_at(group.chips - o) + group.core
        copy = remote(x.at[block], x.at[block], fs.at[o], fr.at[o], group.partner)
        copy.start()
        forwards.append(copy)
    mine.wait()
    for copy in forwards:
        copy.wait()
    save_x = pltpu.make_async_copy(x, vis_out, out_sem.at[0])
    save_x.start()

    def x2d():
        return x[...].reshape(batch, v)

    def finish(area, total):
        field = total + bias[:, area]
        probs_out[:, area] = sigmoid(field).astype(BF16)
        sample = relaxed(field, uni[:, area]).astype(BF16)
        sample_out[:, area] = sample
        return sample

    sub = min(v, 256)

    def consume(t):
        def piece(i, c):
            left = gath[:, :, cols(t * nt, nt)].reshape(batch, nt)
            right = wbuf[lax.rem(t, 2), pl.ds(pl.multiple_of(i * sub, sub), sub), :]
            value = lax.dot_general(left, right, (((1,), (1,)), ((), ())), preferred_element_type=F32)
            area = cols(i * sub, sub)

            @pl.when(t == 0)
            def _():
                acc[:, area] = value

            @pl.when(t > 0)
            def _():
                acc[:, area] = acc[:, area] + value

            return c

        lax.fori_loop(0, v // sub, piece, 0)

    ring_field(ring, x2d, w_hbm, wbuf, wsem, part, recv, gath, rs_sem, ag_sem, ssem, finish, consume)
    save_x.wait()

    def shrink(i, c):
        area = cols(i * sub, sub)
        narrow[:, :, area] = acc[:, area].astype(BF16).reshape(m, rows_c, sub)
        return c

    lax.fori_loop(0, v // sub, shrink, 0)
    save = pltpu.make_async_copy(narrow, part2_out, out_sem.at[1])
    save.start()
    save.wait()


def reconstruct_kernel(
    n, m, part2, uni, bias, probs, recon_out, full_out, probs_out,
    pair, chip_sum, yrecv, rec, gp, ds, dr, ys, yr, gs, gr, ms, mr, fs, fr, ag_sem, ssem, own_sem, out_sem,
):
    ring, group = Ring(n), Group(m)
    rows_c, v = part2.shape[1], part2.shape[2]
    h = gp.shape[2]
    chips = group.chips
    offsets = range(1, chips)
    tiles = dr.shape[0]
    cw = v // tiles
    rtiles = ag_sem.shape[0]
    rnt = h // rtiles
    rw = rnt // 2
    own = pltpu.make_async_copy(probs, gp.at[ring.me], own_sem)
    own.start()
    barrier([ring.peer(0), ring.peer(1), group.partner] + [group.peer(o) for o in offsets])

    def pair_copy(t, y):
        area = cols(t * cw, cw)
        return remote(
            part2.at[2 * y + 1 - group.core, :, area], pair.at[y, :, area], ds.at[t, y], dr.at[t, y], group.partner
        )

    def y_copy(t, o):
        area = cols(t * cw, cw)
        return remote(chip_sum.at[o - 1, :, area], yrecv.at[o - 1, :, area], ys.at[t, o - 1], yr.at[t, o - 1], group.peer(o))

    def g_copy(t, o):
        area = cols(t * cw, cw)
        return remote(
            rec.at[group.me, :, area], rec.at[group.me, :, area], gs.at[t, o - 1], gr.at[t, o - 1], group.peer(o)
        )

    def m_copy(t):
        area = cols(t * cw, cw)
        return remote(rec.at[group.me, :, area], rec.at[group.me, :, area], ms.at[t], mr.at[t], group.partner)

    def f_copy(t, o):
        area = cols(t * cw, cw)
        block = 2 * group.chip_at(chips - o) + group.core
        return remote(rec.at[block, :, area], rec.at[block, :, area], fs.at[t, o - 1], fr.at[t, o - 1], group.partner)

    def ag(t, d, step):
        area = cols(t * rnt + d * rw, rw)
        chunk = ring.ag_chunk(d, step)
        return remote(gp.at[chunk, :, area], gp.at[chunk, :, area], ssem.at[t, d], ag_sem.at[t, d, step], ring.peer(d))

    def pairs(t, c):
        for y in range(chips):
            pair_copy(t, y).start()
        return c

    lax.fori_loop(0, tiles, pairs, 0)
    own.wait()

    def slot(k, carry):
        @pl.when(k < rtiles)
        def _():
            for d in range(2):
                ag(k, d, 0).start()

        @pl.when(k < tiles)
        def _():
            area = cols(k * cw, cw)
            for y in range(chips):
                pair_copy(k, y).wait()
            for o in offsets:
                y = group.chip_at(o)
                total = part2[2 * y + group.core, :, area].astype(F32) + pair[y, :, area].astype(F32)
                chip_sum[o - 1, :, area] = total.astype(BF16)
                y_copy(k, o).start()

        @pl.when((k >= 2) & (k < tiles + 2))
        def _():
            t = k - 2
            area = cols(t * cw, cw)
            total = part2[group.me, :, area].astype(F32) + pair[group.chip, :, area].astype(F32)
            for o in offsets:
                y_copy(t, o).wait()
                total = total + yrecv[o - 1, :, area].astype(F32)
            sample = relaxed(total + bias[:, area], uni[:, area]).astype(BF16)
            recon_out[:, area] = sample
            rec[group.me, :, area] = sample
            for o in offsets:
                g_copy(t, o).start()
            m_copy(t).start()

        @pl.when(k >= 4)
        def _():
            t = k - 4

            @pl.when(t < tiles)
            def _():
                for o in offsets:
                    g_copy(t, o).wait()
                    f_copy(t, o).start()

        def row_tile(t, c):
            j = k - t

            @pl.when((j >= 1) & (j <= n - 2))
            def _():
                for d in range(2):
                    ag(t, d, j - 1).wait()
                    ag(t, d, j).start()

            @pl.when(j == n - 1)
            def _():
                for d in range(2):
                    ag(t, d, n - 2).wait()

            return c

        lax.fori_loop(jnp.maximum(k - (n - 1), 0), jnp.minimum(k + 1, rtiles), row_tile, 0)
        return carry

    lax.fori_loop(0, max(tiles + 4, rtiles + n - 1), slot, 0)
    save_probs = pltpu.make_async_copy(gp, probs_out, out_sem.at[0])
    save_probs.start()

    def drain(t, c):
        m_copy(t).wait()
        for o in offsets:
            f_copy(t, o).wait()
        return c

    lax.fori_loop(0, tiles, drain, 0)
    save_full = pltpu.make_async_copy(rec, full_out, out_sem.at[1])
    save_full.start()
    save_probs.wait()
    save_full.wait()


def negative_kernel(
    n, x, w_hbm, bias, probs_out,
    wbuf, part, recv, gath, wsem, rs_sem, ag_sem, ssem, out_sem,
):
    ring = Ring(n)
    nt = wbuf.shape[2]
    pltpu.make_async_copy(w_hbm.at[:, cols(0, nt)], wbuf.at[0], wsem.at[0]).start()
    barrier([ring.peer(0), ring.peer(1)])

    def finish(area, total):
        return sigmoid(total + bias[:, area]).astype(BF16)

    ring_field(
        ring, lambda: x[...], w_hbm, wbuf, wsem, part, recv, gath, rs_sem, ag_sem, ssem, finish, None
    )
    save = pltpu.make_async_copy(gath, probs_out, out_sem)
    save.start()
    save.wait()


def params(cid):
    return pltpu.CompilerParams(collective_id=cid, has_side_effects=True, vmem_limit_bytes=LIMIT)


def ring_scratch(n, batch, v, h, nt):
    rows = batch // n
    return [
        pltpu.VMEM((2, v, nt), BF16),
        pltpu.VMEM((n, rows, h), BF16),
        pltpu.VMEM((n - 1, rows, h), BF16),
        pltpu.VMEM((n, rows, h), BF16),
    ]


def ring_sems(n, tiles):
    dma = pltpu.SemaphoreType.DMA
    return [dma((2,)), dma((tiles, 2, n - 1)), dma((tiles, 2, n - 1)), dma((tiles, 2))]


def on_device(visible_data, hidden_uniform, visible_uniform, weights, visible_bias, hidden_bias):
    n, m = lax.axis_size("row"), lax.axis_size("col")
    v, h = weights.shape
    rows_c, rows_r = visible_data.shape[0], hidden_uniform.shape[0]
    batch = rows_c * m
    chips = m // 2
    dma = pltpu.SemaphoreType.DMA
    shape = jax.ShapeDtypeStruct
    hbias, vbias = hidden_bias.reshape(1, h), visible_bias.reshape(1, v)
    nt = col_tile(h, 512)
    tiles = h // nt

    sample_own, probs_own, part2, visible_full = pl.pallas_call(
        functools.partial(positive_kernel, n, m),
        name="positive",
        out_shape=[
            shape((rows_r, h), BF16),
            shape((rows_r, h), BF16),
            shape((m, rows_c, v), BF16),
            shape((m, rows_c, v), BF16),
        ],
        in_specs=[ANY, ANY, VM, VM],
        out_specs=[VM, VM, ANY, ANY],
        scratch_shapes=[pltpu.VMEM((m, rows_c, v), BF16)]
        + ring_scratch(n, batch, v, h, nt)
        + [pltpu.VMEM((batch, v), F32), pltpu.VMEM((m, rows_c, v), BF16)]
        + ring_sems(n, tiles)
        + [dma, dma((max(chips - 1, 1),)), dma((max(chips - 1, 1),)), dma((chips,)), dma((chips,)), dma((2,))],
        compiler_params=params(1),
        cost_estimate=pl.CostEstimate(flops=4 * batch * v * h, bytes_accessed=4 * v * h, transcendentals=0),
    )(visible_data, weights, hidden_uniform, hbias)

    cw = col_tile(v, 512)
    vtiles = v // cw
    rtiles = max(1, h // 1024)
    recon_own, recon_full, probs_full = pl.pallas_call(
        functools.partial(reconstruct_kernel, n, m),
        name="reconstruct",
        out_shape=[shape((rows_c, v), BF16), shape((m, rows_c, v), BF16), shape((n, rows_r, h), BF16)],
        in_specs=[VM, VM, VM, ANY],
        out_specs=[VM, ANY, ANY],
        scratch_shapes=[
            pltpu.VMEM((chips, rows_c, v), BF16),
            pltpu.VMEM((max(chips - 1, 1), rows_c, v), BF16),
            pltpu.VMEM((max(chips - 1, 1), rows_c, v), BF16),
            pltpu.VMEM((m, rows_c, v), BF16),
            pltpu.VMEM((n, rows_r, h), BF16),
            dma((vtiles, chips)),
            dma((vtiles, chips)),
        ]
        + [dma((vtiles, max(chips - 1, 1)))] * 4
        + [dma((vtiles,))] * 2
        + [dma((vtiles, max(chips - 1, 1)))] * 2
        + [dma((rtiles, 2, n - 1)), dma((rtiles, 2)), dma, dma((2,))],
        compiler_params=params(2),
        cost_estimate=pl.CostEstimate(flops=2 * batch * v * h, bytes_accessed=8 * batch * v, transcendentals=0),
    )(part2, visible_uniform, vbias, probs_own)

    recon2d = recon_full.reshape(batch, v)
    negative_full = pl.pallas_call(
        functools.partial(negative_kernel, n),
        name="negative",
        out_shape=shape((n, rows_r, h), BF16),
        in_specs=[VM, ANY, VM],
        out_specs=ANY,
        scratch_shapes=ring_scratch(n, batch, v, h, nt) + ring_sems(n, tiles) + [dma],
        compiler_params=params(3),
        cost_estimate=pl.CostEstimate(flops=2 * batch * v * h, bytes_accessed=2 * v * h, transcendentals=0),
    )(recon2d, weights, hbias)

    visible_full = visible_full.reshape(batch, v)
    probs_full, negative_full = probs_full.reshape(batch, h), negative_full.reshape(batch, h)
    left_side = jnp.concatenate([visible_full, recon2d], axis=0)
    right_side = jnp.concatenate([probs_full, -negative_full], axis=0)
    difference = lax.dot_general(
        left_side, right_side, (((0,), (0,)), ((), ())), preferred_element_type=F32
    )
    grad_weights = (difference / batch).astype(BF16)
    grad_visible = jnp.mean(visible_full.astype(F32) - recon2d.astype(F32), axis=0)
    grad_hidden = jnp.mean(probs_full.astype(F32) - negative_full.astype(F32), axis=0)
    return (grad_weights, grad_visible, grad_hidden, sample_own, recon_own)


def solution(mesh):
    placed = (
        P("col", "row"),
        P("row", "col"),
        P("col", "row"),
        P("row", "col"),
        P("row"),
        P("col"),
    )
    return jax.shard_map(
        on_device,
        mesh=mesh,
        in_specs=placed,
        out_specs=(P("row", "col"), P("row"), P("col"), P("row", "col"), P("col", "row")),
        check_vma=False,
    )
```

time: 659 us -> 384 us (0.58)
  waiting for transfers between devices: 507 us -> 0 us
  Pallas kernels: 0 us -> 324 us
  matrix products: 114 us -> 43.7 us
  between operations: 14.2 us -> 0.69 us
  other arithmetic: 22.6 us -> 13.4 us
    pallas_call x0 -> x3, Pallas kernels: none -> 324 us  [the longest x1 163 us: on_device(): pl.pallas_call(functools.partial(positive_kernel, n, m), name='positive',...]
    all_gather x5 -> x0, waiting for transfers between devices: 287 us -> none  [gather(): return lax.all_gather(value, axis, axis=0, tiled=True)]
    reduce_scatter x3 -> x0, waiting for transfers between devices: 219 us -> none  [scatter_sum(): lax.psum_scatter(narrow, axis, scatter_dimension=0, tiled=True)]
    dot_general x4 -> x1, matrix products: 114 us -> 43.7 us  [on_device(): lax.dot_general(left_side, right_side, (((0,), (0,)), ((), ())), preferre...]
    convert_element_type x3 -> x0, other arithmetic: 8.66 us -> none  [the longest x1 3.66 us: on_device(): recon_own = relaxed(field_neg, visible_uniform).astype(jnp.bfloat16)]
  transfers between devices with their start and end apart: 8 -> 0, of which waited for: 8 -> 0; matrix products, arithmetic and copies ran while one was open for 1% -> 0% of each run, Pallas kernels for 0% -> 0%
where the time goes in v1:
time: 384 us; the launch traced here: 383 us
  Pallas kernels  324 us (84%)
  matrix products  43.7 us (11%)
  other arithmetic  13.4 us (3%)
    pallas_call x1, Pallas kernels, on_device(): pl.pallas_call(functools.partial(positive_kernel, n, m), name='positive',...  163 us
    pallas_call x1, Pallas kernels, on_device(): pl.pallas_call(functools.partial(negative_kernel, n), name='negative', ou...  102 us
    pallas_call x1, Pallas kernels, on_device(): pl.pallas_call(functools.partial(reconstruct_kernel, n, m), name='reconst...  58.3 us
    dot_general x1, matrix products, on_device(): lax.dot_general(left_side, right_side, (((0,), (0,)), ((), ())), preferre...  43.7 us

profile of v1, /device:TPU:0, one launch (start us, length us, event | category | flops | bytes accessed | tf_op | source)
XLA Modules:
  0.0 383.4 jit_solution(14243712948772311634)
XLA Ops:
  0.6 163.2 %positive.1 = (bf16[64,4096]{1,0:T(8,128)(2,1)}, bf16[64,4096]{1,0:T(8,128)(2,1)}, bf16[4,128,4096]{2,1,0:T(8,128)(2,1)}, bf16[4,128,4096]{2,1,0:T(8,128)(2,1)}) custom-call(bf16[128,4096]{1,0:T(8,128)(2,1)} %vis.1, bf16[4096,4096]{1,0:T(8,128)(2,1)} %w_hbm.3, f32[64,4096]{1,0:T(8,128)} %uni.2, f32[1,4096]{1,0:T(1,128)} %bitcast.12), custom_call_target="tpu_custom_call" | custom-call | flops 34359738368 | bytes 67108864 | tf_op jit(solution)/shard_map/positive/pallas_call | solution.py:468
  163.9 58.3 %reconstruct.1 = (bf16[128,4096]{1,0:T(8,128)(2,1)}, bf16[4,128,4096]{2,1,0:T(8,128)(2,1)}, bf16[8,64,4096]{2,1,0:T(8,128)(2,1)}) custom-call(bf16[4,128,4096]{2,1,0:T(8,128)(2,1)} %get-tuple-element.13.part2, f32[128,4096]{1,0:T(8,128)} %uni.3, f32[1,4096]{1,0:T(1,128)} %bitcast.11, bf16[64,4096]{1,0:T(8,128)(2,1)} %get-tuple-element.14.probs), custom_call_target="tpu_custom_call" | custom-call | flops 17179869184 | bytes 16777216 | tf_op jit(solution)/shard_map/reconstruct/pallas_call | solution.py:491
  222.2 4.9 %subtract_reduce_fusion.1 = f32[4096]{0:T(1024)S(1)} fusion(bf16[4,128,4096]{2,1,0:T(8,128)(2,1)} %get-tuple-element.15, bf16[4,128,4096]{2,1,0:T(8,128)(2,1)} %get-tuple-element.12), kind=kLoop, calls=%fused_computation.8 | loop fusion | flops 8384512 | bytes 8404992 | tf_op jit(solution)/shard_map/reduce_sum | solution.py:534
  227.1 102.3 %negative.1 = bf16[8,64,4096]{2,1,0:T(8,128)(2,1)} custom-call(bf16[512,4096]{1,0:T(8,128)(2,1)} %bitcast.7, bf16[4096,4096]{1,0:T(8,128)(2,1)} %w_hbm.3, f32[1,4096]{1,0:T(1,128)} %bitcast.13), custom_call_target="tpu_custom_call" | custom-call | flops 17179869184 | bytes 33554432 | tf_op jit(solution)/shard_map/negative/pallas_call | solution.py:515
  329.5 0.0 copy-start
  329.5 5.1 %subtract_reduce_fusion = f32[4096]{0:T(1024)S(1)} fusion(bf16[8,64,4096]{2,1,0:T(8,128)(2,1)} %negative.1, bf16[8,64,4096]{2,1,0:T(8,128)(2,1)} %get-tuple-element.16), kind=kLoop, calls=%fused_computation.7 | loop fusion | flops 8384512 | bytes 8404992 | tf_op jit(solution)/shard_map/reduce_sum | solution.py:535
  334.5 0.0 copy-done
  334.5 2.8 neg.6
  337.3 0.6 broadcast_multiply_fusion
  337.9 0.0 copy-start.2
  337.9 0.0 copy-start.1
  337.9 43.7 %multiply_convert_fusion = bf16[4096,4096]{1,0:T(8,128)(2,1)} fusion(bf16[512,4096]{1,0:T(8,128)(2,1)} %bitcast.8, bf16[512,4096]{1,0:T(8,128)(2,1)} %bitcast.6, bf16[512,4096]{1,0:T(8,128)(2,1)} %bitcast.10, bf16[512,4096]{1,0:T(8,128)(2,1)} %bitcast.9), kind=kOutput, calls=%fused_computation | convolution fusion | flops 34426847232 | bytes 50331648 | tf_op jit(solution)/shard_map/dot_general | solution.py:530
  381.7 0.0 copy-done.2
  381.7 0.8 copy.13
  382.5 0.0 copy-done.1
  382.5 1.0 copy.14
Async XLA Ops:
  329.5 5.1 %copy-start = (bf16[8,64,4096]{2,1,0:T(8,128)(2,1)S(1)}, bf16[8,64,4096]{2,1,0:T(8,128)(2,1)}, u32[]{:S(2)}) copy-start(bf16[8,64,4096]{2,1,0:T(8,128)(2,1)} %negative.1) | copy-start | bytes 12582916
  337.9 43.7 %copy-start.2 = (bf16[64,4096]{1,0:T(8,128)(2,1)S(1)}, bf16[64,4096]{1,0:T(8,128)(2,1)}, u32[]{:S(2)}) copy-start(bf16[64,4096]{1,0:T(8,128)(2,1)} %get-tuple-element.29) | copy-start | bytes 1572868
  337.9 44.5 %copy-start.1 = (bf16[128,4096]{1,0:T(8,128)(2,1)S(1)}, bf16[128,4096]{1,0:T(8,128)(2,1)}, u32[]{:S(2)}) copy-start(bf16[128,4096]{1,0:T(8,128)(2,1)} %get-tuple-element.30) | copy-start | bytes 3145732

commit v2 on v0

v2 whole, which is shorter than its diff:
```python
import functools

import jax
import jax.numpy as jnp
from jax import lax
from jax.experimental import pallas as pl
from jax.experimental.pallas import tpu as pltpu
from jax.sharding import PartitionSpec as P

MESH = pl.DeviceIdType.MESH
BF16 = jnp.bfloat16
F32 = jnp.float32
ANY = pl.BlockSpec(memory_space=pl.ANY)
VM = pl.BlockSpec(memory_space=pltpu.VMEM)
LIMIT = 64_000_000


def sigmoid(t):
    return 1.0 / (1.0 + jnp.exp(-t))


def relaxed(field, uniform):
    return sigmoid(2.0 * (field + jnp.log(uniform) - jnp.log(1.0 - uniform)))


def col_tile(size, want):
    return min(size, want)


class Ring:
    def __init__(self, n):
        self.n = n
        me = lax.axis_index("row")
        self.me = me
        self.col = lax.axis_index("col")
        half, odd = me // 2, me % 2
        self.pos = half + odd * (n - 1 - 2 * half)
        self.right = self.index(self.pos + 1)
        self.left = self.index(self.pos + n - 1)

    def index(self, p):
        p = lax.rem(p, self.n)
        far = p // (self.n // 2)
        return (1 - far) * (2 * p) + far * (2 * (self.n - 1 - p) + 1)

    def peer(self, d):
        return (self.right if d == 0 else self.left, self.col)

    def rs_chunk(self, d, step):
        if d == 0:
            return self.index(self.pos + 2 * self.n - 1 - step)
        return self.index(self.pos + 1 + step)

    def ag_chunk(self, d, step):
        if d == 0:
            return self.index(self.pos + self.n - step)
        return self.index(self.pos + step)


class Group:
    def __init__(self, m):
        self.m = m
        self.chips = m // 2
        self.me = lax.axis_index("col")
        self.row = lax.axis_index("row")
        self.chip, self.core = self.me // 2, self.me % 2
        self.partner = (self.row, 2 * self.chip + 1 - self.core)

    def chip_at(self, offset):
        return lax.rem(self.chip + offset, self.chips)

    def peer(self, offset):
        return (self.row, 2 * self.chip_at(offset) + self.core)


def barrier(devices):
    sem = pltpu.get_barrier_semaphore()
    for device in devices:
        pl.semaphore_signal(sem, inc=1, device_id=device, device_id_type=MESH)
    pl.semaphore_wait(sem, len(devices))


def remote(src, dst, send, recv, device):
    return pltpu.make_async_remote_copy(
        src_ref=src, dst_ref=dst, send_sem=send, recv_sem=recv, device_id=device, device_id_type=MESH
    )


def cols(start, width):
    return pl.ds(pl.multiple_of(start, 128), width)


def add_rows(total, area, block):
    total[:, area] = total[:, area] + jnp.sum(block.astype(F32), axis=0, keepdims=True)


class RingSum:
    def __init__(self, ring, part, recv, gath, rs_sem, ag_sem, ssem):
        self.ring, self.part, self.recv, self.gath = ring, part, recv, gath
        self.rs_sem, self.ag_sem, self.ssem = rs_sem, ag_sem, ssem
        self.tiles = ssem.shape[0]
        self.half = part.shape[2] // 2
        self.w = self.half // self.tiles

    def area(self, t, d):
        return cols(d * self.half + t * self.w, self.w)

    def rs(self, t, d, step):
        area, ring = self.area(t, d), self.ring
        return remote(
            self.part.at[ring.rs_chunk(d, step), :, area],
            self.recv.at[step, :, area],
            self.ssem.at[t, d],
            self.rs_sem.at[t, d, step],
            ring.peer(d),
        )

    def ag(self, t, d, step):
        area, ring = self.area(t, d), self.ring
        block = self.gath.at[ring.ag_chunk(d, step), :, area]
        return remote(block, block, self.ssem.at[t, d], self.ag_sem.at[t, d, step], ring.peer(d))

    def each(self, body):
        def tile(t, c):
            for d in range(2):
                body(t, d, self.area(t, d))
            return c

        lax.fori_loop(0, self.tiles, tile, 0)

    def reduce(self, finish):
        ring, part, recv, gath = self.ring, self.part, self.recv, self.gath
        n = ring.n

        def step(j, c):
            def body(t, d, area):
                self.rs(t, d, j - 1).wait()
                q = ring.rs_chunk(d, j)
                total = part[q, :, area].astype(F32) + recv[j - 1, :, area].astype(F32)
                part[q, :, area] = total.astype(BF16)
                self.rs(t, d, j).start()

            self.each(body)
            return c

        lax.fori_loop(1, n - 1, step, 0)

        def close(t, d, area):
            self.rs(t, d, n - 2).wait()
            total = part[ring.me, :, area].astype(F32) + recv[n - 2, :, area].astype(F32)
            gath[ring.me, :, area] = finish(area, total)
            self.ag(t, d, 0).start()

        self.each(close)

    def gather(self, arrived, between):
        n = self.ring.n

        def step(s, c):
            def body(t, d, area):
                self.ag(t, d, s).wait()
                self.ag(t, d, s + 1).start()
                if arrived is not None:
                    arrived(area, self.gath[self.ring.ag_chunk(d, s + 1), :, area])

            self.each(body)
            if between is not None:
                between(s)
            return c

        lax.fori_loop(0, n - 2, step, 0)

        def close(t, d, area):
            self.ag(t, d, n - 2).wait()
            if arrived is not None:
                arrived(area, self.gath[self.ring.ag_chunk(d, n - 1), :, area])

        self.each(close)


PIECES = 4


def positive_kernel(
    n, m, vis, w_hbm, uni, bias, sample_out, probs_out, vsum_out, part2_out, vis_out,
    x, wbuf, part, recv, gath, acc, narrow, wsem, rs_sem, ag_sem, ssem, own_sem, gs, gr, fs, fr, ms, mr, out_sem,
):
    ring, group = Ring(n), Group(m)
    rows_c, rows_r = x.shape[1], part.shape[1]
    v, h = x.shape[2], part.shape[2]
    vb = v // PIECES
    chips = group.chips
    pair = 2 * rows_c
    chunks = pair // rows_r
    offsets = range(1, chips)
    sub = min(vb, h, 256)

    def load(i):
        block = lax.rem(i, PIECES)
        return pltpu.make_async_copy(
            w_hbm.at[pl.ds(pl.multiple_of(block * vb, vb), vb), :], wbuf.at[lax.rem(i, 2)], wsem.at[lax.rem(i, 2)]
        )

    load(0).start()
    load(1).start()
    own = pltpu.make_async_copy(vis, x.at[group.me], own_sem)
    own.start()
    barrier([ring.peer(0), ring.peer(1), group.partner] + [group.peer(o) for o in offsets])
    own.wait()

    def y_copy(o, p):
        block = x.at[group.me, :, cols(p * vb, vb)]
        return remote(block, block, gs.at[o - 1, p], gr.at[o - 1, p], group.peer(o))

    def f_copy(o, p):
        block = x.at[2 * group.chip_at(chips - o) + group.core, :, cols(p * vb, vb)]
        return remote(block, block, fs.at[o - 1, p], fr.at[o - 1, p], group.partner)

    mine = remote(x.at[group.me], x.at[group.me], ms, mr, group.partner)
    mine.start()
    for p in range(PIECES):
        for o in offsets:
            y_copy(o, p).start()

    sums = RingSum(ring, part, recv, gath, rs_sem, ag_sem, ssem)

    def dot_piece(chip, p, i, width, after):
        rows = pl.ds(pl.multiple_of(chip * pair, pair), pair)

        def piece(start):
            left = x[pl.ds(2 * chip, 2), :, cols(p * vb, vb)].reshape(pair, vb)
            value = jnp.dot(left, wbuf[i % 2, :, cols(start, sub)], preferred_element_type=F32)
            area = cols(start, sub)
            if p > 0:
                value = value + acc[rows, area]
            if p < PIECES - 1:
                acc[rows, area] = value
            else:
                part[pl.ds(chip * chunks, chunks), :, area] = value.astype(BF16).reshape(chunks, rows_r, sub)

        def tile(t, c):
            for d in range(2):

                def one(g, e):
                    piece(d * sums.half + t * width + g * sub)
                    return e

                lax.fori_loop(0, width // sub, one, 0)
                if after:
                    sums.rs(t, d, 0).start()
            return c

        lax.fori_loop(0, sums.half // width, tile, 0)

    mine.wait()
    for p in range(PIECES):
        load(p).wait()
        dot_piece(group.chip, p, p, sums.w, False)
        load(p + 2).start()
        if p == 1:
            for o in offsets:
                y_copy(o, 0).wait()
                f_copy(o, 0).start()
    for p in range(PIECES):
        if p + 1 < PIECES:
            for o in offsets:
                y_copy(o, p + 1).wait()
                f_copy(o, p + 1).start()
        i = PIECES + p
        load(i).wait()
        for o in offsets:
            f_copy(o, p).wait()
            dot_piece(group.chip_at(chips - o), p, i, sums.w, p == PIECES - 1 and o == chips - 1)
        load(i + 2).start()
    save_x = pltpu.make_async_copy(x, vis_out, out_sem.at[0])
    save_x.start()

    vsub = min(v, 256)

    def clear(i, c):
        area = cols(i * vsub, vsub)
        acc[:, area] = jnp.zeros((acc.shape[0], vsub), F32)
        vsum_out[:, area] = jnp.sum(x[:, :, area].astype(F32).reshape(m * rows_c, vsub), axis=0, keepdims=True)
        return c

    lax.fori_loop(0, v // vsub, clear, 0)

    def finish(area, total):
        field = total + bias[:, area]
        probs_out[:, area] = sigmoid(field).astype(BF16)
        sample = relaxed(field, uni[:, area]).astype(BF16)
        sample_out[:, area] = sample
        return sample

    many = n // 2

    def second(block, slot, base):
        psub = min(vb, 256)

        def piece(g, c):
            for d in range(2):
                ids = [ring.ag_chunk(d, base + i) for i in range(many)]
                k = pl.ds(d * sums.half, sums.half)
                left = jnp.concatenate([gath[q, :, k] for q in ids], axis=0)
                right = wbuf[slot, pl.ds(pl.multiple_of(g * psub, psub), psub), k]
                value = lax.dot_general(left, right, (((1,), (1,)), ((), ())), preferred_element_type=F32)
                area = cols(block * vb + g * psub, psub)
                for i, q in enumerate(ids):
                    rows = pl.ds(pl.multiple_of(q * rows_r, rows_r), rows_r)
                    acc[rows, area] = acc[rows, area] + value[i * rows_r : (i + 1) * rows_r, :]
            return c

        lax.fori_loop(0, vb // psub, piece, 0)

    def between(s):
        i = s - (many - 2)

        @pl.when((i >= 0) & (i < PIECES))
        def _():
            load(i).wait()
            second(i, lax.rem(i, 2), 0)
            load(i + 2).start()

    sums.reduce(finish)
    sums.gather(None, between)

    def save(i):
        area = cols(i * vb, vb)
        return pltpu.make_async_copy(narrow.at[:, :, area], part2_out.at[:, :, area], out_sem.at[1 + i])

    for i in range(PIECES):
        load(i).wait()
        second(i, i % 2, many)
        if i + 2 < PIECES:
            load(i + 2).start()

        def shrink(g, c):
            area = cols(i * vb + g * sub, sub)
            narrow[:, :, area] = acc[:, area].astype(BF16).reshape(m, rows_c, sub)
            return c

        lax.fori_loop(0, vb // sub, shrink, 0)
        save(i).start()
    save_x.wait()
    for i in range(PIECES):
        save(i).wait()


def negative_kernel(
    n, m, part2, uni, bias, hbias, vsum, probs, w_hbm, recon_out, gv_out, gh_out, full_out, probs_out, neg_out,
    pair, chip_sum, yrecv, rec, gp, wbuf, acc, part, recv, gath, hsum, rsum,
    ds, dr, ys, yr, gs, gr, fs, fr, ms, mr, agp_sem, agp_send, wsem, rs_sem, ag_sem, ssem, own_sem, out_sem,
):
    ring, group = Ring(n), Group(m)
    rows_c, v = part2.shape[1], part2.shape[2]
    rows_r, h = gp.shape[1], gp.shape[2]
    batch = m * rows_c
    chips = group.chips
    offsets = range(1, chips)
    tiles = dr.shape[0]
    cw = v // tiles
    rtiles = agp_sem.shape[0]
    rnt = h // rtiles
    rw = rnt // 2
    own = pltpu.make_async_copy(probs, gp.at[ring.me], own_sem)
    own.start()

    def load(t):
        return pltpu.make_async_copy(
            w_hbm.at[pl.ds(pl.multiple_of(t * cw, cw), cw), :], wbuf.at[lax.rem(t, 2)], wsem.at[lax.rem(t, 2)]
        )

    load(0).start()
    barrier([ring.peer(0), ring.peer(1), group.partner] + [group.peer(o) for o in offsets])

    def pair_copy(t, y):
        area = cols(t * cw, cw)
        return remote(
            part2.at[2 * y + 1 - group.core, :, area], pair.at[y, :, area], ds.at[t, y], dr.at[t, y], group.partner
        )

    def y_copy(t, o):
        area = cols(t * cw, cw)
        return remote(
            chip_sum.at[o - 1, :, area], yrecv.at[o - 1, :, area], ys.at[t, o - 1], yr.at[t, o - 1], group.peer(o)
        )

    def g_copy(t, o):
        block = rec.at[group.me, :, cols(t * cw, cw)]
        return remote(block, block, gs.at[t, o - 1], gr.at[t, o - 1], group.peer(o))

    def m_copy(t):
        block = rec.at[group.me, :, cols(t * cw, cw)]
        return remote(block, block, ms.at[t], mr.at[t], group.partner)

    def f_copy(t, o):
        block = rec.at[2 * group.chip_at(chips - o) + group.core, :, cols(t * cw, cw)]
        return remote(block, block, fs.at[t, o - 1], fr.at[t, o - 1], group.partner)

    def ag(t, d, step):
        block = gp.at[ring.ag_chunk(d, step), :, cols(t * rnt + d * rw, rw)]
        return remote(block, block, agp_send.at[t, d], agp_sem.at[t, d, step], ring.peer(d))

    def pairs(t, c):
        for y in range(chips):
            pair_copy(t, y).start()
        return c

    lax.fori_loop(0, tiles, pairs, 0)
    own.wait()
    hsum[...] = jnp.zeros_like(hsum)
    rsum[...] = jnp.zeros_like(rsum)
    sub = min(h, 256)

    def slot(k, carry):
        @pl.when(k < rtiles)
        def _():
            for d in range(2):
                ag(k, d, 0).start()
                area = cols(k * rnt + d * rw, rw)
                add_rows(hsum, area, gp[ring.me, :, area])

        @pl.when(k < tiles)
        def _():
            area = cols(k * cw, cw)
            for y in range(chips):
                pair_copy(k, y).wait()
            for o in offsets:
                y = group.chip_at(o)
                total = part2[2 * y + group.core, :, area].astype(F32) + pair[y, :, area].astype(F32)
                chip_sum[o - 1, :, area] = total.astype(BF16)
                y_copy(k, o).start()

        @pl.when((k >= 2) & (k < tiles + 2))
        def _():
            t = k - 2
            area = cols(t * cw, cw)
            total = part2[group.me, :, area].astype(F32) + pair[group.chip, :, area].astype(F32)
            for o in offsets:
                y_copy(t, o).wait()
                total = total + yrecv[o - 1, :, area].astype(F32)
            sample = relaxed(total + bias[:, area], uni[:, area]).astype(BF16)
            recon_out[:, area] = sample
            rec[group.me, :, area] = sample
            for o in offsets:
                g_copy(t, o).start()
            m_copy(t).start()

        @pl.when((k >= 4) & (k < tiles + 4))
        def _():
            for o in offsets:
                g_copy(k - 4, o).wait()
                f_copy(k - 4, o).start()

        def row_tile(t, c):
            j = k - t
            for d in range(2):
                area = cols(t * rnt + d * rw, rw)

                @pl.when(j >= 1)
                def _():
                    ag(t, d, j - 1).wait()

                    @pl.when(j <= n - 2)
                    def _():
                        ag(t, d, j).start()

                    add_rows(hsum, area, gp[ring.ag_chunk(d, j), :, area])

            return c

        lax.fori_loop(jnp.maximum(k - (n - 1), 0), jnp.minimum(k + 1, rtiles), row_tile, 0)

        @pl.when((k >= 5) & (k < tiles + 5))
        def _():
            t = k - 5
            area = cols(t * cw, cw)

            @pl.when(t + 1 < tiles)
            def _():
                load(t + 1).start()

            m_copy(t).wait()
            for o in offsets:
                f_copy(t, o).wait()
            load(t).wait()

            def piece(g, c):
                out = cols(g * sub, sub)
                left = rec[:, :, area].reshape(batch, cw)
                value = jnp.dot(left, wbuf[lax.rem(t, 2), :, out], preferred_element_type=F32)

                @pl.when(t == 0)
                def _():
                    acc[:, out] = value

                @pl.when(t > 0)
                def _():
                    acc[:, out] = acc[:, out] + value

                return c

            lax.fori_loop(0, h // sub, piece, 0)
            add_rows(rsum, area, rec[:, :, area].reshape(batch, cw))

        return carry

    lax.fori_loop(0, max(tiles + 5, rtiles + n - 1), slot, 0)

    sums = RingSum(ring, part, recv, gath, rs_sem, ag_sem, ssem)

    def begin(t, d, area):
        part[:, :, area] = acc[:, area].astype(BF16).reshape(n, rows_r, sums.w)
        sums.rs(t, d, 0).start()

    sums.each(begin)
    save_probs = pltpu.make_async_copy(gp, probs_out, out_sem.at[0])
    save_probs.start()
    save_full = pltpu.make_async_copy(rec, full_out, out_sem.at[1])
    save_full.start()
    gv_out[...] = (vsum[...] - rsum[...]) * (1.0 / batch)

    def finish(area, total):
        value = -sigmoid(total + hbias[:, area]).astype(BF16)
        add_rows(hsum, area, value)
        return value

    def arrived(area, block):
        add_rows(hsum, area, block)

    sums.reduce(finish)
    sums.gather(arrived, None)
    save_neg = pltpu.make_async_copy(gath, neg_out, out_sem.at[2])
    save_neg.start()
    gh_out[...] = hsum[...] * (1.0 / batch)
    save_probs.wait()
    save_full.wait()
    save_neg.wait()


def params(cid):
    return pltpu.CompilerParams(collective_id=cid, has_side_effects=True, vmem_limit_bytes=LIMIT)


def on_device(visible_data, hidden_uniform, visible_uniform, weights, visible_bias, hidden_bias):
    n, m = lax.axis_size("row"), lax.axis_size("col")
    v, h = weights.shape
    rows_c, rows_r = visible_data.shape[0], hidden_uniform.shape[0]
    batch = rows_c * m
    chips = m // 2
    others = max(chips - 1, 1)
    dma = pltpu.SemaphoreType.DMA
    shape = jax.ShapeDtypeStruct
    hbias, vbias = hidden_bias.reshape(1, h), visible_bias.reshape(1, v)
    tiles = (h // 2) // col_tile(h // 2, 512)
    by_row, by_col = (n, rows_r, h), (m, rows_c, v)
    ring_buffers = [pltpu.VMEM(by_row, BF16), pltpu.VMEM((n - 1, rows_r, h), BF16), pltpu.VMEM(by_row, BF16)]
    ring_sems = [dma((tiles, 2, n - 1)), dma((tiles, 2, n - 1)), dma((tiles, 2))]

    sample_own, probs_own, vsum, part2, visible_full = pl.pallas_call(
        functools.partial(positive_kernel, n, m),
        name="positive",
        out_shape=[
            shape((rows_r, h), BF16),
            shape((rows_r, h), BF16),
            shape((1, v), F32),
            shape(by_col, BF16),
            shape(by_col, BF16),
        ],
        in_specs=[ANY, ANY, VM, VM],
        out_specs=[VM, VM, VM, ANY, ANY],
        scratch_shapes=[pltpu.VMEM(by_col, BF16), pltpu.VMEM((2, v // PIECES, h), BF16)]
        + ring_buffers
        + [pltpu.VMEM((batch, max(v, h)), F32), pltpu.VMEM(by_col, BF16), dma((2,))]
        + ring_sems
        + [dma]
        + [dma((others, PIECES))] * 4
        + [dma, dma, dma((1 + PIECES,))],
        compiler_params=params(1),
        cost_estimate=pl.CostEstimate(flops=4 * batch * v * h, bytes_accessed=8 * v * h, transcendentals=0),
    )(visible_data, weights, hidden_uniform, hbias)

    cw = col_tile(v, 512)
    vtiles = v // cw
    rtiles = max(1, h // 1024)
    recon_own, grad_visible, grad_hidden, recon_full, probs_full, negative_full = pl.pallas_call(
        functools.partial(negative_kernel, n, m),
        name="negative",
        out_shape=[
            shape((rows_c, v), BF16),
            shape((1, v), F32),
            shape((1, h), F32),
            shape(by_col, BF16),
            shape(by_row, BF16),
            shape(by_row, BF16),
        ],
        in_specs=[VM, VM, VM, VM, VM, ANY, ANY],
        out_specs=[VM, VM, VM, ANY, ANY, ANY],
        scratch_shapes=[
            pltpu.VMEM((chips, rows_c, v), BF16),
            pltpu.VMEM((others, rows_c, v), BF16),
            pltpu.VMEM((others, rows_c, v), BF16),
            pltpu.VMEM(by_col, BF16),
            pltpu.VMEM(by_row, BF16),
            pltpu.VMEM((2, cw, h), BF16),
            pltpu.VMEM((batch, h), F32),
        ]
        + ring_buffers
        + [pltpu.VMEM((1, h), F32), pltpu.VMEM((1, v), F32)]
        + [dma((vtiles, chips))] * 2
        + [dma((vtiles, others))] * 6
        + [dma((vtiles,))] * 2
        + [dma((rtiles, 2, n - 1)), dma((rtiles, 2)), dma((2,))]
        + ring_sems
        + [dma, dma((3,))],
        compiler_params=params(2),
        cost_estimate=pl.CostEstimate(flops=2 * batch * v * h, bytes_accessed=2 * v * h, transcendentals=0),
    )(part2, visible_uniform, vbias, hbias, vsum, probs_own, weights)

    left_side = jnp.concatenate([visible_full, recon_full], axis=0).reshape(2 * batch, v)
    right_side = jnp.concatenate([probs_full, negative_full], axis=0).reshape(2 * batch, h)
    difference = lax.dot_general(
        left_side, right_side, (((0,), (0,)), ((), ())), preferred_element_type=F32
    )
    grad_weights = (difference / batch).astype(BF16)
    return (grad_weights, grad_visible.reshape(v), grad_hidden.reshape(h), sample_own, recon_own)


def solution(mesh):
    placed = (
        P("col", "row"),
        P("row", "col"),
        P("col", "row"),
        P("row", "col"),
        P("row"),
        P("col"),
    )
    return jax.shard_map(
        on_device,
        mesh=mesh,
        in_specs=placed,
        out_specs=(P("row", "col"), P("row"), P("col"), P("row", "col"), P("col", "row")),
        check_vma=False,
    )
```

time: 659 us -> 373 us (0.57)
  waiting for transfers between devices: 507 us -> 0 us
  Pallas kernels: 0 us -> 311 us
  matrix products: 114 us -> 43.7 us
  between operations: 14.2 us -> 0.66 us
  other arithmetic: 22.6 us -> 14.8 us
    pallas_call x0 -> x2, Pallas kernels: none -> 311 us  [the longest x1 165 us: on_device(): pl.pallas_call(functools.partial(negative_kernel, n, m), name='negative',...]
    all_gather x5 -> x0, waiting for transfers between devices: 287 us -> none  [gather(): return lax.all_gather(value, axis, axis=0, tiled=True)]
    reduce_scatter x3 -> x0, waiting for transfers between devices: 219 us -> none  [scatter_sum(): lax.psum_scatter(narrow, axis, scatter_dimension=0, tiled=True)]
    dot_general x4 -> x1, matrix products: 114 us -> 43.7 us  [on_device(): lax.dot_general(left_side, right_side, (((0,), (0,)), ((), ())), preferre...]
    concatenate x0 -> x2, other arithmetic: none -> 14.8 us  [the longest x1 7.42 us: on_device(): jnp.concatenate([visible_full, recon_full], axis=0).reshape(2 * batch, v)]
    reduce_sum x2 -> x0, other arithmetic: 9.97 us -> none  [the longest x1 5.05 us: on_device(): jnp.mean(probs_full.astype(jnp.float32) - negative_full.astype(jnp.float3...]
    convert_element_type x3 -> x0, other arithmetic: 8.66 us -> none  [the longest x1 3.66 us: on_device(): recon_own = relaxed(field_neg, visible_uniform).astype(jnp.bfloat16)]
  transfers between devices with their start and end apart: 8 -> 0, of which waited for: 8 -> 0; matrix products, arithmetic and copies ran while one was open for 1% -> 0% of each run, Pallas kernels for 0% -> 0%
where the time goes in v2:
time: 373 us
  Pallas kernels  311 us (83%)
  matrix products  43.7 us (12%)
  other arithmetic  14.8 us (4%)
    pallas_call x1, Pallas kernels, on_device(): pl.pallas_call(functools.partial(negative_kernel, n, m), name='negative',...  165 us
    pallas_call x1, Pallas kernels, on_device(): pl.pallas_call(functools.partial(positive_kernel, n, m), name='positive',...  146 us
    dot_general x1, matrix products, on_device(): lax.dot_general(left_side, right_side, (((0,), (0,)), ((), ())), preferre...  43.7 us

profile of v2, /device:TPU:0, one launch (start us, length us, event | category | flops | bytes accessed | tf_op | source)
XLA Modules:
  0.0 373.0 jit_solution(1922371567459776760)
XLA Ops:
  0.6 146.2 %positive.1 = (bf16[64,4096]{1,0:T(8,128)(2,1)}, bf16[64,4096]{1,0:T(8,128)(2,1)}, f32[1,4096]{1,0:T(1,128)}, bf16[4,128,4096]{2,1,0:T(8,128)(2,1)}, bf16[4,128,4096]{2,1,0:T(8,128)(2,1)}) custom-call(bf16[128,4096]{1,0:T(8,128)(2,1)} %vis.1, bf16[4096,4096]{1,0:T(8,128)(2,1)} %w_hbm.3, f32[64,4096]{1,0:T(8,128)} %uni.2, f32[1,4096]{1,0:T(1,128)} %bitcast.12), custom_call_target="tpu_custom_call" | custom-call | flops 34359738368 | bytes 134217728 | tf_op jit(solution)/shard_map/positive/pallas_call | solution.py:560
  146.8 164.7 %negative.1 = (bf16[128,4096]{1,0:T(8,128)(2,1)}, f32[1,4096]{1,0:T(1,128)}, f32[1,4096]{1,0:T(1,128)}, bf16[4,128,4096]{2,1,0:T(8,128)(2,1)}, bf16[8,64,4096]{2...) custom-call(bf16[4,128,4096]{2,1,0:T(8,128)(2,1)} %get-tuple-element.17.part2, f32[128,4096]{1,0:T(8,128)} %uni.3, ...), custom_call_target="tpu_custom_call" | custom-call | flops 17179869184 | bytes 33554432 | tf_op jit(solution)/shard_map/negative/pallas_call | solution.py:586
  311.5 7.4 %pad_maximum_fusion = bf16[8,128,4096]{2,1,0:T(8,128)(2,1)} fusion(bf16[4,128,4096]{2,1,0:T(8,128)(2,1)} %get-tuple-element.20, bf16[4,128,4096]{2,1,0:T(8,128)(2,1)} %get-tuple-element.16), kind=kLoop, calls=%fused_computation.1 | loop fusion | flops 4194304 | bytes 16777216 | tf_op jit(solution)/shard_map/concatenate | solution.py:620
  318.9 7.4 %pad_maximum_fusion.1 = bf16[16,64,4096]{2,1,0:T(8,128)(2,1)} fusion(bf16[8,64,4096]{2,1,0:T(8,128)(2,1)} %get-tuple-element.22, bf16[8,64,4096]{2,1,0:T(8,128)(2,1)} %get-tuple-element.21), kind=kLoop, calls=%fused_computation.2 | loop fusion | flops 4194304 | bytes 16777216 | tf_op jit(solution)/shard_map/concatenate | solution.py:621
  326.3 0.0 copy-start.3
  326.3 0.0 copy-start.2
  326.3 0.0 copy-start.1
  326.4 0.0 copy-start
  326.4 43.7 %multiply_convert_fusion = bf16[4096,4096]{1,0:T(8,128)(2,1)} fusion(bf16[1024,4096]{1,0:T(8,128)(2,1)} %bitcast.8, bf16[1024,4096]{1,0:T(8,128)(2,1)} %bitcast.9), kind=kOutput, calls=%fused_computation | convolution fusion | flops 34393292800 | bytes 50331648 | tf_op jit(solution)/shard_map/dot_general | solution.py:622
  370.0 0.0 copy-done.3
  370.0 0.6 copy.15
  370.6 0.0 copy-done.2
  370.6 0.6 copy.16
  371.3 0.0 copy-done.1
  371.3 0.8 copy.17
  372.1 0.0 copy-done
  372.1 1.0 copy.18
Async XLA Ops:
  326.3 43.7 %copy-start.3 = (f32[1,4096]{1,0:T(1,128)S(1)}, f32[1,4096]{1,0:T(1,128)}, u32[]{:S(2)}) copy-start(f32[1,4096]{1,0:T(1,128)} %get-tuple-element.23) | copy-start | bytes 49156
  326.3 44.3 %copy-start.2 = (f32[1,4096]{1,0:T(1,128)S(1)}, f32[1,4096]{1,0:T(1,128)}, u32[]{:S(2)}) copy-start(f32[1,4096]{1,0:T(1,128)} %get-tuple-element.24) | copy-start | bytes 49156
  326.3 44.9 %copy-start.1 = (bf16[64,4096]{1,0:T(8,128)(2,1)S(1)}, bf16[64,4096]{1,0:T(8,128)(2,1)}, u32[]{:S(2)}) copy-start(bf16[64,4096]{1,0:T(8,128)(2,1)} %get-tuple-element.35) | copy-start | bytes 1572868
  326.4 45.7 %copy-start = (bf16[128,4096]{1,0:T(8,128)(2,1)S(1)}, bf16[128,4096]{1,0:T(8,128)(2,1)}, u32[]{:S(2)}) copy-start(bf16[128,4096]{1,0:T(8,128)(2,1)} %get-tuple-element.36) | copy-start | bytes 3145732
